TPU v7x, 32 devices: a whole 2x2x4 slice. The times are simulated.
32 devices in a mesh: seq: 8 (over z, x), head: 4 (over y, core).
Axes of the slice: x: 2, y: 2, z: 4, core: 2. Of those that a mesh axis runs over, the one named last changes fastest.
Arguments:
- queries: bfloat16 [4096, 4096], P('seq', 'head'), may hold values from -6 to 6
- keys: bfloat16 [4096, 4096], P('seq', 'head'), may hold values from -6 to 6
- values: bfloat16 [4096, 4096], P('seq', 'head'), may hold values from -6 to 6
- med_weight: float32 [2, 32, 4], P(None, 'head'), may hold values from -3 to 3
- coarse_weight: float32 [2, 32, 64], P(None, 'head'), may hold values from -0.75 to 0.75
- out_weight: bfloat16 [4096, 4096], P('head'), may hold values from -0.09375 to 0.09375
Outputs:
- mixed: bfloat16 [4096, 4096], P('seq', 'head')
All inputs are finite; a program needn't handle non-finite values.
Results may differ from a plain program's by a relative error of at most 0.013.
Values may be sent and summed in bfloat16 or wider, within the bound.
A program may use at most 128 MiB of HBM per device.

v0:
```python
import math

import jax
import jax.numpy as jnp
from jax import lax
from jax.sharding import PartitionSpec as P

HEAD_DIM = 128
WIN = 512
MED = 4
COARSE = 64


def shifted(block, axis, distance):
    devices = range(lax.axis_size(axis))
    route = [(i - distance, i) for i in devices if i - distance in devices]
    return lax.ppermute(block, axis, route)


def summarize(tensor, weight, ratio):
    groups = tensor.shape[0] // ratio
    grouped = tensor.reshape(groups, ratio, tensor.shape[1], tensor.shape[2]).astype(jnp.float32)
    return jnp.einsum("jrhd,hr->jhd", grouped, weight).astype(jnp.bfloat16)


def attend_block(query_blk, query_place, key_all, value_all, key_place, usable, score_scale):
    scores = (
        jnp.einsum("qhd,khd->hqk", query_blk, key_all, preferred_element_type=jnp.float32)
        * score_scale
    )
    allowed = (key_place[None, :] <= query_place[:, None]) & usable[None, :]
    scores = jnp.where(allowed[None], scores, -jnp.inf)
    row_peak = jnp.max(scores, axis=-1)
    exp_scores = jnp.exp(scores - row_peak[..., None])
    row_total = jnp.sum(exp_scores, axis=-1)
    weighted = jnp.einsum(
        "hqk,khd->hqd",
        exp_scores.astype(jnp.bfloat16),
        value_all,
        preferred_element_type=jnp.float32,
    )
    return (row_peak, row_total, weighted)


def body(queries, keys, values, med_weight, coarse_weight, out_weight):
    tok_rows = queries.shape[0]
    head_count = queries.shape[1] // HEAD_DIM
    flat_width = head_count * HEAD_DIM
    score_scale = 1.0 / math.sqrt(HEAD_DIM)
    position = lax.axis_index("seq")
    query3 = queries.reshape(tok_rows, head_count, HEAD_DIM)
    key3 = keys.reshape(tok_rows, head_count, HEAD_DIM)
    value3 = values.reshape(tok_rows, head_count, HEAD_DIM)
    edge_keys, edge_values = shifted((keys, values), "seq", 1)
    edge_keys = edge_keys.reshape(WIN, head_count, HEAD_DIM)
    edge_values = edge_values.reshape(WIN, head_count, HEAD_DIM)
    med_keys = summarize(key3, med_weight[0], MED).reshape(-1, flat_width)
    med_values = summarize(value3, med_weight[1], MED).reshape(-1, flat_width)
    coarse_keys = summarize(key3, coarse_weight[0], COARSE).reshape(-1, flat_width)
    coarse_values = summarize(value3, coarse_weight[1], COARSE).reshape(-1, flat_width)
    moved = shifted((med_keys, med_values), "seq", 2)
    fetched = [moved]
    for distance in (3, 4):
        moved = shifted((moved[0], moved[1]), "seq", 1)
        fetched.append(moved)
    key_list = [key3]
    value_list = [value3]
    place_list = [jnp.arange(tok_rows, dtype=jnp.int32)]
    usable_list = [jnp.ones((tok_rows,), bool)]
    key_list.append(edge_keys)
    value_list.append(edge_values)
    place_list.append(jnp.full((WIN,), -1, jnp.int32))
    usable_list.append(jnp.broadcast_to(position >= 1, (WIN,)))
    for distance, fetched_pair in zip((2, 3, 4), fetched):
        med_rows = fetched_pair[0].shape[0]
        key_list.append(fetched_pair[0].reshape(med_rows, head_count, HEAD_DIM))
        value_list.append(fetched_pair[1].reshape(med_rows, head_count, HEAD_DIM))
        place_list.append(jnp.full((med_rows,), -1, jnp.int32))
        usable_list.append(jnp.broadcast_to(position >= distance, (med_rows,)))
    per_coarse = tok_rows // COARSE
    gathered_keys, gathered_values = (
        lax.all_gather(coarse_keys, "seq", axis=0, tiled=True),
        lax.all_gather(coarse_values, "seq", axis=0, tiled=True),
    )
    rows_all = gathered_keys.shape[0]
    key_list.append(gathered_keys.reshape(rows_all, head_count, HEAD_DIM))
    value_list.append(gathered_values.reshape(rows_all, head_count, HEAD_DIM))
    place_list.append(jnp.full((rows_all,), -1, jnp.int32))
    usable_list.append(jnp.arange(rows_all, dtype=jnp.int32) // per_coarse <= position - 1)
    key_all = jnp.concatenate(key_list, 0)
    value_all = jnp.concatenate(value_list, 0)
    key_place = jnp.concatenate(place_list, 0)
    usable = jnp.concatenate(usable_list, 0)
    block_rows = math.gcd(tok_rows, 512)
    block_count = tok_rows // block_rows
    query_blocks = query3.reshape(block_count, block_rows, head_count, HEAD_DIM)

    def local_pass(index):
        query_place = index * block_rows + jnp.arange(block_rows, dtype=jnp.int32)
        return attend_block(
            query_blocks[index], query_place, key_all, value_all, key_place, usable, score_scale
        )

    row_peak, row_total, weighted = lax.map(local_pass, jnp.arange(block_count, dtype=jnp.int32))
    row_peak = row_peak.transpose(1, 0, 2).reshape(head_count, tok_rows)
    row_total = row_total.transpose(1, 0, 2).reshape(head_count, tok_rows)
    weighted = weighted.transpose(1, 0, 2, 3).reshape(head_count, tok_rows, HEAD_DIM)
    attention = (weighted / row_total[..., None]).astype(jnp.bfloat16)
    attention = attention.transpose(1, 0, 2).reshape(tok_rows, flat_width)
    partial_sum = jnp.dot(attention, out_weight, preferred_element_type=jnp.float32)
    rounded = lax.optimization_barrier(partial_sum.astype(jnp.bfloat16)).astype(jnp.float32)
    mixed = lax.psum_scatter(rounded.astype(jnp.bfloat16), "head", scatter_dimension=1, tiled=True)
    return mixed


def solution(mesh):
    placed = (
        P("seq", "head"),
        P("seq", "head"),
        P("seq", "head"),
        P(None, "head", None),
        P(None, "head", None),
        P("head", None),
    )
    return jax.shard_map(
        body, mesh=mesh, in_specs=placed, out_specs=P("seq", "head"), check_vma=False
    )
```

profile of v0, /device:TPU:19, one launch (start us, length us, event | category | flops | bytes accessed | tf_op | source)
XLA Modules:
  0.0 258.2 jit_solution(8200015731911551215)
XLA Ops:
  12.1 1.8 copy.30
  13.9 3.2 %collective-permute-start.1 = (bf16[128,1024]{0,1:T(8,128)(2,1)}, bf16[128,1024]{0,1:T(8,128)(2,1)}, u32[]{:S(2)}, u32[]{:S(2)}) collective-permute-start(bf16[128,1024]{0,1:T(8,128)(2,1)} %bitcast.101), channel_id=1, source_target_pairs={{0,8},{4,12},{8,16},{12,20},{16,24},{20,28},{1,9},{5,13},{9,17},{1... | collective-permute-start | bytes 786440 | tf_op jit(solution)/shard_map/ppermute | solution.py:17
  18.0 1.9 collective-permute-start.5
  19.9 2.3 copy.17
  22.2 1.9 collective-permute-start.4
  24.1 2.3 copy.8
  26.4 1.9 collective-permute-start
  29.8 1.8 fusion.5
  31.9 56.5 %all_gather.7 = bf16[64,1024]{1,0:T(8,128)(2,1)S(1)} all-gather(bf16[8,1024]{1,0:T(8,128)(2,1)S(1)} %convert_bitcast_fusion), channel_id=1, replica_groups=mesh['seq'=8,'head'=4] {'seq'}, dimensions={0}, use_global_device_ids=true | all-gather | bytes 147456 | tf_op jit(solution)/shard_map/all_gather | solution.py:83
  88.5 2.3 copy.19
  92.3 5.4 %collective-permute-start.2 = (bf16[128,1024]{0,1:T(8,128)(2,1)}, bf16[128,1024]{0,1:T(8,128)(2,1)S(1)}, u32[]{:S(2)}, u32[]{:S(2)}) collective-permute-start(bf16[128,1024]{0,1:T(8,128)(2,1)} %collective-permute-done.1), channel_id=1, source_target_pairs={{0,4},{4,8},{8,12},{12,16},{16,20},{20,24},{24,28},{1,5},{5,9},{9,... | collective-permute-start | bytes 786440 | tf_op jit(solution)/shard_map/ppermute | solution.py:17
  97.8 2.7 %collective-permute-start.6 = (bf16[128,1024]{0,1:T(8,128)(2,1)S(1)}, bf16[128,1024]{0,1:T(8,128)(2,1)S(1)}, u32[]{:S(2)}, u32[]{:S(2)}) collective-permute-start(bf16[128,1024]{0,1:T(8,128)(2,1)S(1)} %collective-permute-done.5), channel_id=1, source_target_pairs={{0,4},{4,8},{8,12},{12,16},{16,20},{20,24},{24,28},{1,5},{5,9},{9,... | collective-permute-start | bytes 786440 | tf_op jit(solution)/shard_map/ppermute | solution.py:17
  100.5 22.9 %all_gather.6 = bf16[64,1024]{1,0:T(8,128)(2,1)} all-gather(bf16[8,1024]{1,0:T(8,128)(2,1)S(1)} %convert_bitcast_fusion.1), channel_id=1, replica_groups=mesh['seq'=8,'head'=4] {'seq'}, dimensions={0}, use_global_device_ids=true | all-gather | bytes 147456 | tf_op jit(solution)/shard_map/all_gather | solution.py:82
  123.4 4.0 %collective-permute-start.3 = (bf16[128,1024]{0,1:T(8,128)(2,1)S(1)}, bf16[128,1024]{0,1:T(8,128)(2,1)S(1)}, u32[]{:S(2)}, u32[]{:S(2)}) collective-permute-start(bf16[128,1024]{0,1:T(8,128)(2,1)S(1)} %collective-permute-done.2), channel_id=1, source_target_pairs={{0,4},{4,8},{8,12},{12,16},{16,20},{20,24},{24,28},{1,5},{5,9},{9,... | collective-permute-start | bytes 786440 | tf_op jit(solution)/shard_map/ppermute | solution.py:17
  127.4 4.1 %collective-permute-start.7 = (bf16[128,1024]{0,1:T(8,128)(2,1)S(1)}, bf16[128,1024]{0,1:T(8,128)(2,1)S(1)}, u32[]{:S(2)}, u32[]{:S(2)}) collective-permute-start(bf16[128,1024]{0,1:T(8,128)(2,1)S(1)} %collective-permute-done.6), channel_id=1, source_target_pairs={{0,4},{4,8},{8,12},{12,16},{16,20},{20,24},{24,28},{1,5},{5,9},{9,... | collective-permute-start | bytes 786440 | tf_op jit(solution)/shard_map/ppermute | solution.py:17
  131.5 2.4 constant_dynamic-update-slice_fusion.5
  135.1 1.8 copy.12
  141.4 2.3 copy.11
  143.7 2.6 constant_dynamic-update-slice_fusion.4
  155.0 9.9 %fusion.17 = (f32[8,512]{1,0:T(8,128)S(1)}, f32[8,512,1472]{1,2,0:T(8,128)}) fusion(bf16[1472,8,128]{2,0,1:T(8,128)(2,1)S(1)} %copy-done.1, pred[512,1472]{0,1:T(8,128)(4,1)S(1)} %copy-done.2, bf16[512,1024]{1,0:T(8,128)(2,1)S(1)} %copy-done), kind=kOutput, calls=%fused_computation.46 | convolution fusion | flops 1561587712 | bytes 28950528 | tf_op jit(solution)/shard_map/while/body/eval_jaxpr/qhd,khd->hqk/dot_general | solution.py:28
  164.9 10.0 %fusion = f32[8,512]{1,0:T(8,128)S(1)} fusion(f32[8,512,1472]{1,2,0:T(8,128)} %get-tuple-element.32, f32[8,512]{1,0:T(8,128)S(1)} %get-tuple-element.23), kind=kLoop, calls=%fused_computation.2 | loop fusion | flops 12054528 | bytes 24150016 | tf_op jit(solution)/shard_map/while/body/eval_jaxpr/reduce_sum | solution.py:35
  174.9 10.1 %fusion.6 = bf16[512,8,128]{0,2,1:T(8,128)(2,1)S(1)} fusion(bf16[1472,8,128]{2,0,1:T(8,128)(2,1)S(1)} %bitcast_dynamic-update-slice_fusion, f32[8,512,1472]{1,2,0:T(8,128)} %get-tuple-element.32, f32[8,512]{1,0:T(8,128)S(1)} %get-tuple-element.23, f32[512,8]{0,1:T(8,128)S(1)} %bitcast.110), kind=kOutput, calls=%fused_computation.10 | convolution fusion | flops 1556611072 | bytes 28213248 | tf_op jit(solution)/shard_map/while/body/eval_jaxpr/hqk,khd->hqd/dot_general | solution.py:36
  184.9 9.5 %convolution_convert_fusion = bf16[512,4096]{1,0:T(8,128)(2,1)} fusion(bf16[512,1024]{0,1:T(8,128)(2,1)S(1)} %bitcast.111, bf16[1024,4096]{1,0:T(8,128)(2,1)} %param.11), kind=kOutput, calls=%fused_computation.6 | convolution fusion | flops 4297064448 | bytes 13631488 | tf_op jit(solution)/shard_map/dot_general | solution.py:110
  194.5 56.9 %reduce-scatter.2.cloned.1.call-done = bf16[512,1024]{1,0:T(8,128)(2,1)} async-done(((bf16[512,4096]{1,0:T(8,128)(2,1)}), bf16[512,1024]{1,0:T(8,128)(2,1)}) %reduce-scatter.2.cloned.1.call-update) | async-done | bytes 1048592 | tf_op jit(solution)/shard_map/reduce_scatter | solution.py:112
  (72 shorter events, 24.1 us)
Async XLA Ops:
  6.5 146.9 %copy-start = (bf16[512,1024]{1,0:T(8,128)(2,1)S(1)}, bf16[512,1024]{1,0:T(8,128)(2,1)}, u32[]{:S(2)}) copy-start(bf16[512,1024]{1,0:T(8,128)(2,1)} %param.6) | copy-start | bytes 3145732
  6.5 244.8 %reduce-scatter.2.cloned.1.call-start = ((), (), s32[]{:S(2)}) async-start(), calls=%async_computation.1 | async-start | bytes 5242880 | tf_op jit(solution)/shard_map/reduce_scatter | solution.py:112
  12.1 16.4 %copy-start.7 = (f32[2,8,64]{2,1,0:T(8,128)S(1)}, f32[2,8,64]{2,1,0:T(8,128)}, u32[]{:S(2)}) copy-start(f32[2,8,64]{2,1,0:T(8,128)} %param.10) | copy-start | bytes 12292
  13.9 78.5 %collective-permute-start.1 = (bf16[128,1024]{0,1:T(8,128)(2,1)}, bf16[128,1024]{0,1:T(8,128)(2,1)}, u32[]{:S(2)}, u32[]{:S(2)}) collective-permute-start(bf16[128,1024]{0,1:T(8,128)(2,1)} %bitcast.101), channel_id=1, source_target_pairs={{0,8},{4,12},{8,16},{12,20},{16,24},{20,28},{1,9},{5,13},{9,17},{1... | collective-permute-start | bytes 786440 | tf_op jit(solution)/shard_map/ppermute | solution.py:17
  18.0 79.8 %collective-permute-start.5 = (bf16[128,1024]{0,1:T(8,128)(2,1)}, bf16[128,1024]{0,1:T(8,128)(2,1)S(1)}, u32[]{:S(2)}, u32[]{:S(2)}) collective-permute-start(bf16[128,1024]{0,1:T(8,128)(2,1)} %bitcast.100), channel_id=1, source_target_pairs={{0,8},{4,12},{8,16},{12,20},{16,24},{20,28},{1,9},{5,13},{9,17},{1... | collective-permute-start | bytes 786440 | tf_op jit(solution)/shard_map/ppermute | solution.py:17
  22.2 117.6 %collective-permute-start.4 = (bf16[512,1024]{0,1:T(8,128)(2,1)}, bf16[512,1024]{0,1:T(8,128)(2,1)}, u32[]{:S(2)}, u32[]{:S(2)}) collective-permute-start(bf16[512,1024]{0,1:T(8,128)(2,1)} %copy.17), channel_id=1, source_target_pairs={{0,4},{4,8},{8,12},{12,16},{16,20},{20,24},{24,28},{1,5},{5,9},{9,... | collective-permute-start | bytes 3145736 | tf_op jit(solution)/shard_map/ppermute | solution.py:17
  26.4 115.0 %collective-permute-start = (bf16[512,1024]{0,1:T(8,128)(2,1)}, bf16[512,1024]{0,1:T(8,128)(2,1)}, u32[]{:S(2)}, u32[]{:S(2)}) collective-permute-start(bf16[512,1024]{0,1:T(8,128)(2,1)} %copy.8), channel_id=1, source_target_pairs={{0,4},{4,8},{8,12},{12,16},{16,20},{20,24},{24,28},{1,5},{5,9},{9,... | collective-permute-start | bytes 3145736 | tf_op jit(solution)/shard_map/ppermute | solution.py:17
  31.9 58.8 %copy-start.3 = (bf16[512,1024]{0,1:T(8,128)(2,1)S(1)}, bf16[512,1024]{0,1:T(8,128)(2,1)}, u32[]{:S(2)}) copy-start(bf16[512,1024]{0,1:T(8,128)(2,1)} %copy.8) | copy-start | bytes 3145732
  92.1 41.9 %copy-start.4 = (bf16[512,8,128]{2,0,1:T(8,128)(2,1)S(1)}, bf16[512,8,128]{2,0,1:T(8,128)(2,1)}, u32[]{:S(2)}) copy-start(bf16[512,8,128]{2,0,1:T(8,128)(2,1)} %copy.19) | copy-start | bytes 3145732
  92.3 31.0 %collective-permute-start.2 = (bf16[128,1024]{0,1:T(8,128)(2,1)}, bf16[128,1024]{0,1:T(8,128)(2,1)S(1)}, u32[]{:S(2)}, u32[]{:S(2)}) collective-permute-start(bf16[128,1024]{0,1:T(8,128)(2,1)} %collective-permute-done.1), channel_id=1, source_target_pairs={{0,4},{4,8},{8,12},{12,16},{16,20},{20,24},{24,28},{1,5},{5,9},{9,... | collective-permute-start | bytes 786440 | tf_op jit(solution)/shard_map/ppermute | solution.py:17
  97.8 29.6 %collective-permute-start.6 = (bf16[128,1024]{0,1:T(8,128)(2,1)S(1)}, bf16[128,1024]{0,1:T(8,128)(2,1)S(1)}, u32[]{:S(2)}, u32[]{:S(2)}) collective-permute-start(bf16[128,1024]{0,1:T(8,128)(2,1)S(1)} %collective-permute-done.5), channel_id=1, source_target_pairs={{0,4},{4,8},{8,12},{12,16},{16,20},{20,24},{24,28},{1,5},{5,9},{9,... | collective-permute-start | bytes 786440 | tf_op jit(solution)/shard_map/ppermute | solution.py:17
  123.4 14.7 %collective-permute-start.3 = (bf16[128,1024]{0,1:T(8,128)(2,1)S(1)}, bf16[128,1024]{0,1:T(8,128)(2,1)S(1)}, u32[]{:S(2)}, u32[]{:S(2)}) collective-permute-start(bf16[128,1024]{0,1:T(8,128)(2,1)S(1)} %collective-permute-done.2), channel_id=1, source_target_pairs={{0,4},{4,8},{8,12},{12,16},{16,20},{20,24},{24,28},{1,5},{5,9},{9,... | collective-permute-start | bytes 786440 | tf_op jit(solution)/shard_map/ppermute | solution.py:17
  127.4 11.5 %collective-permute-start.7 = (bf16[128,1024]{0,1:T(8,128)(2,1)S(1)}, bf16[128,1024]{0,1:T(8,128)(2,1)S(1)}, u32[]{:S(2)}, u32[]{:S(2)}) collective-permute-start(bf16[128,1024]{0,1:T(8,128)(2,1)S(1)} %collective-permute-done.6), channel_id=1, source_target_pairs={{0,4},{4,8},{8,12},{12,16},{16,20},{20,24},{24,28},{1,5},{5,9},{9,... | collective-permute-start | bytes 786440 | tf_op jit(solution)/shard_map/ppermute | solution.py:17
  143.7 9.5 %copy-start.6 = (bf16[1472,8,128]{2,0,1:T(8,128)(2,1)S(1)}, bf16[1472,8,128]{2,0,1:T(8,128)(2,1)}, u32[]{:S(2)}) copy-start(bf16[1472,8,128]{2,0,1:T(8,128)(2,1)} %constant_dynamic-update-slice_fusion.10) | copy-start | bytes 9043972
  146.2 7.1 %copy-start.5 = (bf16[128,8,128]{2,0,1:T(8,128)(2,1)S(1)}, bf16[128,8,128]{2,0,1:T(8,128)(2,1)}, u32[]{:S(2)}) copy-start(bf16[128,8,128]{2,0,1:T(8,128)(2,1)} %copy.23) | copy-start | bytes 786436
  146.2 7.2 %copy-start.2 = (pred[512,1472]{0,1:T(8,128)(4,1)S(1)}, pred[512,1472]{0,1:T(8,128)(4,1)}, u32[]{:S(2)}) copy-start(pred[512,1472]{0,1:T(8,128)(4,1)} %fusion.5) | copy-start | bytes 2260996
  153.1 1.9 copy-start.1
Sparse Core Ops, SparseCore 0:
  194.6 56.6 reduce-scatter.1
where the time goes:
time: 261 us; the launch traced here: 258 us
  blocking collectives  79.4 us (30%)
  waiting for transfers between devices  56.9 us (22%)
  local copies, waits for them, and re-layouts  39.4 us (15%)
  matrix products  30 us (11%)
  starting transfers between devices  25.1 us (10%)
  between operations  13.7 us (5%)
  other arithmetic  13.6 us (5%)
    reduce_scatter x1, waiting for transfers between devices, body(): lax.psum_scatter(rounded.astype(jnp.bfloat16), 'head', scatter_dimension=...  56.9 us
    all_gather x1, blocking collectives, body(): lax.all_gather(coarse_values, 'seq', axis=0, tiled=True)  56.5 us
    ppermute x8, starting transfers between devices, shifted(): return lax.ppermute(block, axis, route)  25.1 us
    all_gather x1, blocking collectives, body(): lax.all_gather(coarse_keys, 'seq', axis=0, tiled=True)  22.9 us
    unnamed x39, local copies, waits for them, and re-layouts  21.9 us
    dot_general x1, matrix products, attend_block(): jnp.einsum('hqk,khd->hqd', exp_scores.astype(jnp.bfloat16), value_all, pr...  10.1 us
    reduce_sum x1, other arithmetic, attend_block(): row_total = jnp.sum(exp_scores, axis=-1)  10 us
    dot_general x1, matrix products, attend_block(): jnp.einsum('qhd,khd->hqk', query_blk, key_all, preferred_element_type=jnp...  9.89 us
  transfers between devices with their start and end apart: 9, of which 1 were waited for; matrix products, arithmetic and copies ran while one was open for 9% of the time, Pallas kernels for 0%

commit v1 on v0

v1 whole, which is shorter than its diff:
```python
import functools
import math

import jax
import jax.numpy as jnp
from jax import lax
from jax.experimental import pallas as pl
from jax.experimental.pallas import tpu as pltpu
from jax.sharding import PartitionSpec as P

HEAD_DIM = 128
MED = 4
COARSE = 64
CHUNKS = 2
MESH = pl.DeviceIdType.MESH
F32 = jnp.float32
BF16 = jnp.bfloat16


def mm(a, b):
    return jnp.dot(a, b, preferred_element_type=F32)


def mm_nt(a, b):
    return lax.dot_general(a, b, (((1,), (1,)), ((), ())), preferred_element_type=F32)


def split(w):
    hi = w.astype(BF16)
    return hi, (w - hi.astype(F32)).astype(BF16)


def kernel(
    n_seq, n_head, q_hbm, k_hbm, v_hbm, wm_ref, wc_ref, w_hbm, out_ref,
    q_v, k_v, v_v, w_v, vt, q_in, oe_out, le_out, oe_in, le_in,
    med_own, med_in, c_own, c_in, ck, cvt, o_loc, m_loc, l_loc, attn,
    pair_out, pair_in, far_out, far_in, acc,
    ld_sem, q_ss, q_rs, oe_ss, oe_rs, le_ss, le_rs, med_ss, med_rs, c_ss, c_rs,
    pair_ss, pair_rs, far_ss, far_rs,
):
    tok, feat = q_v.shape
    heads = feat // HEAD_DIM
    chunk = tok // CHUNKS
    n_med = tok // MED
    n_coarse = tok // COARSE
    width = out_ref.shape[1]
    scale = 1.0 / math.sqrt(HEAD_DIM)
    pos = lax.axis_index("seq")
    hd = lax.axis_index("head")
    groups = n_head // 2
    grp = hd // 2
    core = lax.rem(hd, 2)
    mate = grp * 2 + (1 - core)

    def remote(src, dst, ss, rs, **dev):
        return pltpu.make_async_remote_copy(
            src_ref=src, dst_ref=dst, send_sem=ss, recv_sem=rs,
            device_id=dev, device_id_type=MESH,
        )

    def hs(h):
        return pl.ds(pl.multiple_of(h * HEAD_DIM, HEAD_DIM), HEAD_DIM)

    loads = [
        pltpu.make_async_copy(s, d, ld_sem.at[n])
        for n, (s, d) in enumerate(((k_hbm, k_v), (v_hbm, v_v), (q_hbm, q_v), (w_hbm, w_v)))
    ]
    for ld in loads:
        ld.start()

    barrier = pltpu.get_barrier_semaphore()

    @pl.loop(1, n_seq)
    def _(d):
        pl.semaphore_signal(
            barrier, inc=1, device_id={"seq": lax.rem(pos + d, n_seq)}, device_id_type=MESH
        )

    @pl.loop(1, n_head)
    def _(d):
        pl.semaphore_signal(
            barrier, inc=1, device_id={"head": lax.rem(hd + d, n_head)}, device_id_type=MESH
        )

    @pl.loop(0, n_seq)
    def _(o):
        @pl.when(o >= pos)
        def _():
            c_in[o] = jnp.zeros(c_in.shape[1:], BF16)

    for slot in range(3):
        @pl.when(pos < slot + 2)
        def _():
            med_in[slot] = jnp.zeros(med_in.shape[1:], BF16)

    @pl.when(pos == 0)
    def _():
        oe_in[...] = jnp.zeros_like(oe_in)
        le_in[...] = jnp.full_like(le_in, -jnp.inf)

    pl.semaphore_wait(barrier, n_seq - 1 + n_head - 1)

    def q_copy(i):
        rows = pl.ds(i * chunk, chunk)
        return remote(
            q_hbm.at[rows], q_in.at[i], q_ss.at[i], q_rs.at[i], seq=jnp.maximum(pos - 1, 0)
        )

    def oe_copy(i, h):
        return remote(
            oe_out.at[i, h], oe_in.at[i, h], oe_ss.at[i, h], oe_rs.at[i, h],
            seq=jnp.minimum(pos + 1, n_seq - 1),
        )

    def le_copy(i):
        return remote(
            le_out.at[i], le_in.at[i], le_ss.at[i], le_rs.at[i],
            seq=jnp.minimum(pos + 1, n_seq - 1),
        )

    def med_copy(slot):
        src = med_own if slot == 0 else med_in.at[0]
        step = (2, 1, 2)[slot]
        return remote(
            src, med_in.at[slot], med_ss.at[slot], med_rs.at[slot],
            seq=jnp.minimum(pos + step, n_seq - 1),
        )

    def c_copy(to):
        return remote(c_own, c_in.at[pos], c_ss.at[to], c_rs.at[pos], seq=to)

    has_prev = pos >= 1
    has_next = pos < n_seq - 1

    @pl.when(has_prev)
    def _():
        for i in range(CHUNKS):
            q_copy(i).start()

    loads[0].wait()
    loads[1].wait()

    @pl.loop(0, heads)
    def _(h):
        kh = k_v[:, hs(h)]
        vh = v_v[:, hs(h)]
        vth = vh.T
        vt[h] = vth
        row = lax.broadcasted_iota(jnp.int32, (n_med, tok), 0)
        col = lax.broadcasted_iota(jnp.int32, (n_med, tok), 1)
        pick = (col // MED) == row
        hi, lo = split(jnp.where(pick, wm_ref[h], 0.0))
        med_own[0, h] = (mm(hi, kh) + mm(lo, kh)).astype(BF16)
        hi, lo = split(jnp.where(pick, wm_ref[heads + h], 0.0))
        med_own[1, h] = (mm_nt(vth, hi) + mm_nt(vth, lo)).astype(BF16)
        row = lax.broadcasted_iota(jnp.int32, (2 * n_coarse, tok), 0)
        col = lax.broadcasted_iota(jnp.int32, (2 * n_coarse, tok), 1) // COARSE
        hi, lo = split(jnp.where(col == row, wc_ref[h], 0.0))
        hi2, lo2 = split(jnp.where(col + n_coarse == row, wc_ref[heads + h], 0.0))
        c_own[h] = (mm(hi, kh) + mm(lo, kh) + mm(hi2, vh) + mm(lo2, vh)).astype(BF16)

    @pl.when(pos + 2 < n_seq)
    def _():
        med_copy(0).start()

    @pl.loop(0, n_seq)
    def _(to):
        @pl.when(to > pos)
        def _():
            c_copy(to).start()

    def edge(i):
        @pl.when(has_next)
        def _():
            q_copy(i).wait_recv()

            @pl.loop(0, heads)
            def _(h):
                s = mm_nt(k_v[:, hs(h)], q_in[i, :, hs(h)])
                m = jnp.max(s, axis=0, keepdims=True)
                p = jnp.exp((s - m) * scale)
                total = jnp.sum(p, axis=0, keepdims=True)
                o = mm(vt[h], p.astype(BF16))
                oe_out[i, h] = (o / total).astype(BF16)
                le_out[i, h] = m * scale + jnp.log(total)
                oe_copy(i, h).start()

            le_copy(i).start()

    def local(i):
        keys = (i + 1) * chunk
        first = i * chunk

        @pl.loop(0, heads)
        def _(h):
            q = q_v[pl.ds(first, chunk), hs(h)]
            s = mm_nt(k_v[pl.ds(0, keys), hs(h)], q)
            key_at = lax.broadcasted_iota(jnp.int32, (keys, chunk), 0)
            query_at = lax.broadcasted_iota(jnp.int32, (keys, chunk), 1) + first
            parts = [(jnp.where(key_at <= query_at, s, -jnp.inf), vt[h, :, pl.ds(0, keys)])]
            for slot in range(3):
                s = mm_nt(med_in[slot, 0, h], q)
                parts.append((jnp.where(pos >= slot + 2, s, -jnp.inf), med_in[slot, 1, h]))
            s = mm_nt(ck[h], q)
            owner = lax.broadcasted_iota(jnp.int32, s.shape, 0) // n_coarse
            parts.append((jnp.where(owner < pos, s, -jnp.inf), cvt[h]))
            m = functools.reduce(
                jnp.maximum, [jnp.max(s, axis=0, keepdims=True) for s, _ in parts]
            )
            total = 0.0
            o = 0.0
            for s, vals in parts:
                p = jnp.exp((s - m) * scale)
                total = total + jnp.sum(p, axis=0, keepdims=True)
                o = o + mm(vals, p.astype(BF16))
            o_loc[i, h] = o
            m_loc[i, h] = m * scale
            l_loc[i, h] = total

    def combine(i):
        @pl.when(has_prev)
        def _():
            le_copy(i).wait_recv()

            @pl.loop(0, heads)
            def _(h):
                oe_copy(i, h).wait_recv()

        @pl.loop(0, heads)
        def _(h):
            lse = le_in[i, h]
            top = jnp.maximum(m_loc[i, h], lse)
            a = jnp.exp(m_loc[i, h] - top)
            e = jnp.exp(lse - top)
            inv = 1.0 / (l_loc[i, h] * a + e)
            o = o_loc[i, h] * (a * inv) + oe_in[i, h].astype(F32) * (e * inv)
            attn[i, :, hs(h)] = o.T.astype(BF16)

    tile = math.gcd(width, 512)

    def project(i, target, put):
        @pl.loop(0, width // tile)
        def _(j):
            cols = pl.ds(pl.multiple_of(target * width + j * tile, tile), tile)
            put(pl.ds(pl.multiple_of(j * tile, tile), tile), mm(attn[i], w_v[:, cols]))

    def pair_copy(i, o):
        return remote(
            pair_out.at[i, o], pair_in.at[i, o], pair_ss.at[i, o], pair_rs.at[i, o], head=mate
        )

    def far_copy(i, o):
        return remote(
            far_out.at[i, o - 1], far_in.at[i, o - 1], far_ss.at[i, o - 1], far_rs.at[i, o - 1],
            head=lax.rem(grp + o, groups) * 2 + core,
        )

    def mix(i):
        order = list(range(1, groups)) + [0]
        for o in order:
            there = lax.rem(grp + o, groups) * 2

            def put_pair(cols, value):
                pair_out[i, o, :, cols] = value.astype(BF16)

            project(i, there + (1 - core), put_pair)
            pair_copy(i, o).start()
            if o:
                def put_far(cols, value):
                    acc[i, :, cols] = value

                project(i, there + core, put_far)
                pair_copy(i, o).wait_recv()
                far_out[i, o - 1] = (acc[i] + pair_in[i, o].astype(F32)).astype(BF16)
                far_copy(i, o).start()

        def put_own(cols, value):
            acc[i, :, cols] = value

        project(i, hd, put_own)

    edge(0)

    @pl.when(pos >= 2)
    def _():
        med_copy(0).wait_recv()

        @pl.when(has_next)
        def _():
            med_copy(1).start()

        @pl.when(pos + 2 < n_seq)
        def _():
            med_copy(2).start()

    for i in range(1, CHUNKS):
        edge(i)

    @pl.loop(0, n_seq)
    def _(o):
        @pl.when(o < pos)
        def _():
            remote(c_own, c_in.at[o], c_ss.at[o], c_rs.at[o], seq=o).wait_recv()

    @pl.loop(0, heads)
    def _(h):
        got = c_in[:, h].astype(F32)
        ck[h] = got[:, :n_coarse].reshape(n_seq * n_coarse, HEAD_DIM).astype(BF16)
        cvt[h] = got[:, n_coarse:].reshape(n_seq * n_coarse, HEAD_DIM).T.astype(BF16)

    loads[2].wait()
    for slot in (1, 2):
        @pl.when(pos >= slot + 2)
        def _():
            med_copy(slot).wait_recv()

    for i in range(CHUNKS):
        local(i)
    loads[3].wait()
    for i in range(CHUNKS):
        combine(i)
        mix(i)
    for i in range(CHUNKS):
        pair_copy(i, 0).wait_recv()
        total = acc[i] + pair_in[i, 0].astype(F32)
        for o in range(1, groups):
            far_copy(i, o).wait_recv()
            total = total + far_in[i, o - 1].astype(F32)
        out_ref[pl.ds(i * chunk, chunk), :] = total.astype(BF16)

    @pl.when(has_prev)
    def _():
        for i in range(CHUNKS):
            q_copy(i).wait_send()

    @pl.when(has_next)
    def _():
        for i in range(CHUNKS):
            le_copy(i).wait_send()

            @pl.loop(0, heads)
            def _(h):
                oe_copy(i, h).wait_send()

    @pl.when(pos + 2 < n_seq)
    def _():
        med_copy(0).wait_send()

    @pl.when((pos >= 2) & has_next)
    def _():
        med_copy(1).wait_send()

    @pl.when((pos >= 2) & (pos + 2 < n_seq))
    def _():
        med_copy(2).wait_send()

    @pl.loop(0, n_seq)
    def _(to):
        @pl.when(to > pos)
        def _():
            c_copy(to).wait_send()

    for i in range(CHUNKS):
        for o in range(groups):
            pair_copy(i, o).wait_send()
            if o:
                far_copy(i, o).wait_send()


def body(n_seq, n_head, queries, keys, values, med_weight, coarse_weight, out_weight):
    tok, feat = queries.shape
    heads = feat // HEAD_DIM
    chunk = tok // CHUNKS
    width = out_weight.shape[1] // n_head
    groups = n_head // 2
    far = max(groups - 1, 1)
    n_med = tok // MED
    n_coarse = tok // COARSE
    wm = jnp.tile(med_weight, (1, 1, n_med)).reshape(2 * heads, 1, tok)
    wc = jnp.tile(coarse_weight, (1, 1, n_coarse)).reshape(2 * heads, 1, tok)
    dma = pltpu.SemaphoreType.DMA
    hbm = pl.BlockSpec(memory_space=pl.ANY)
    vmem = pl.BlockSpec(memory_space=pltpu.VMEM)
    V = pltpu.VMEM
    scratch = [
        V((tok, feat), BF16), V((tok, feat), BF16), V((tok, feat), BF16),
        V(out_weight.shape, BF16),
        V((heads, HEAD_DIM, tok), BF16),
        V((CHUNKS, chunk, feat), BF16),
        V((CHUNKS, heads, HEAD_DIM, chunk), BF16),
        V((CHUNKS, heads, 1, chunk), F32),
        V((CHUNKS, heads, HEAD_DIM, chunk), BF16),
        V((CHUNKS, heads, 1, chunk), F32),
        V((2, heads, n_med, HEAD_DIM), BF16),
        V((3, 2, heads, n_med, HEAD_DIM), BF16),
        V((heads, 2 * n_coarse, HEAD_DIM), BF16),
        V((n_seq, heads, 2 * n_coarse, HEAD_DIM), BF16),
        V((heads, n_seq * n_coarse, HEAD_DIM), BF16),
        V((heads, HEAD_DIM, n_seq * n_coarse), BF16),
        V((CHUNKS, heads, HEAD_DIM, chunk), F32),
        V((CHUNKS, heads, 1, chunk), F32),
        V((CHUNKS, heads, 1, chunk), F32),
        V((CHUNKS, chunk, feat), BF16),
        V((CHUNKS, groups, chunk, width), BF16),
        V((CHUNKS, groups, chunk, width), BF16),
        V((CHUNKS, far, chunk, width), BF16),
        V((CHUNKS, far, chunk, width), BF16),
        V((CHUNKS, chunk, width), F32),
        dma((4,)),
        dma((CHUNKS,)), dma((CHUNKS,)),
        dma((CHUNKS, heads)), dma((CHUNKS, heads)),
        dma((CHUNKS,)), dma((CHUNKS,)),
        dma((3,)), dma((3,)),
        dma((n_seq,)), dma((n_seq,)),
        dma((CHUNKS, groups)), dma((CHUNKS, groups)),
        dma((CHUNKS, far)), dma((CHUNKS, far)),
    ]
    return pl.pallas_call(
        functools.partial(kernel, n_seq, n_head),
        out_shape=jax.ShapeDtypeStruct((tok, width), BF16),
        in_specs=[hbm, hbm, hbm, vmem, vmem, hbm],
        out_specs=vmem,
        scratch_shapes=scratch,
        compiler_params=pltpu.CompilerParams(
            collective_id=0, has_side_effects=True, vmem_limit_bytes=60 * 1024 * 1024
        ),
    )(queries, keys, values, wm, wc, out_weight)


def solution(mesh):
    placed = (
        P("seq", "head"),
        P("seq", "head"),
        P("seq", "head"),
        P(None, "head", None),
        P(None, "head", None),
        P("head", None),
    )
    return jax.shard_map(
        functools.partial(body, mesh.shape["seq"], mesh.shape["head"]),
        mesh=mesh, in_specs=placed, out_specs=P("seq", "head"), check_vma=False,
    )
```

time: 261 us -> 108 us (0.41); the launches traced: 258 us -> 108 us
  Pallas kernels: 0 us -> 102 us
  blocking collectives: 79.4 us -> 0 us
  waiting for transfers between devices: 56.9 us -> 0 us
  local copies, waits for them, and re-layouts: 39.4 us -> 5.51 us
  matrix products: 30 us -> 0 us
  starting transfers between devices: 25.1 us -> 0 us
  between operations: 13.7 us -> 0.02 us
  other arithmetic: 13.6 us -> 0 us
    pallas_call x0 -> x1, Pallas kernels: none -> 102 us  [body(): pl.pallas_call(functools.partial(kernel, n_seq, n_head), out_shape=jax.Sh...]
    all_gather x2 -> x0, blocking collectives: 79.4 us -> none  [the longest x1 56.5 us: body(): lax.all_gather(coarse_values, 'seq', axis=0, tiled=True)]
    reduce_scatter x1 -> x0, waiting for transfers between devices: 56.9 us -> none  [body(): lax.psum_scatter(rounded.astype(jnp.bfloat16), 'head', scatter_dimension=...]
    dot_general x5 -> x0, matrix products: 30 us -> none  [the longest x1 10.1 us: attend_block(): jnp.einsum('hqk,khd->hqd', exp_scores.astype(jnp.bfloat16), value_all, pr...]
    ppermute x8 -> x0, starting transfers between devices: 25.1 us -> none  [shifted(): return lax.ppermute(block, axis, route)]
    unnamed x39 -> x2, local copies, waits for them, and re-layouts: 21.9 us -> 2.95 us
    reshape x10 -> x0, local copies, waits for them, and re-layouts: 12.2 us -> none  [the longest x3 3.51 us: body(): key_list.append(fetched_pair[0].reshape(med_rows, head_count, HEAD_DIM))]
    reduce_sum x1 -> x0, other arithmetic: 10 us -> none  [attend_block(): row_total = jnp.sum(exp_scores, axis=-1)]
  transfers between devices with their start and end apart: 9 -> 0, of which waited for: 1 -> 0; matrix products, arithmetic and copies ran while one was open for 9% -> 0% of each run, Pallas kernels for 0% -> 0%
where the time goes in v1:
time: 108 us
  Pallas kernels  102 us (94%)
  local copies, waits for them, and re-layouts  5.51 us (5%)
    pallas_call x1, Pallas kernels, body(): pl.pallas_call(functools.partial(kernel, n_seq, n_head), out_shape=jax.Sh...  102 us
    unnamed x2, local copies, waits for them, and re-layouts  2.95 us

profile of v1, /device:TPU:19, one launch (start us, length us, event | category | flops | bytes accessed | tf_op | source)
XLA Modules:
  0.0 107.9 jit_solution(320191791390699633)
XLA Ops:
  0.0 0.7 copy.8
  0.7 0.7 tile.18
  1.4 0.7 tile.19.wc_ref
  2.1 0.1 tile.16
  2.2 0.3 tile.17
  2.5 0.7 copy.9.wm_ref
  3.3 102.4 %shard_map.64 = bf16[512,1024]{1,0:T(8,128)(2,1)} custom-call(bf16[512,1024]{1,0:T(8,128)(2,1)} %q_hbm.1, bf16[512,1024]{1,0:T(8,128)(2,1)} %k_hbm.1, bf16[512,1024]{1,0:T(8,128)(2,1)} %v_hbm.1, f32[16,1,512]{2,1,0:T(1,128)} %copy.9.wm_ref, f32[16,1,512]{2,1,0:T(1,128)} %tile.19.wc_ref, bf16[1024,4096]{1,0:T(8,128)(2,1)} %w_hbm.1), custom_call_target="tpu_custom_call" | custom-call | tf_op jit(solution)/shard_map/pallas_call | solution.py:418
  105.7 2.3 %copy.11 = bf16[512,1024]{1,0:T(8,128)(2,1)} copy(bf16[512,1024]{1,0:T(8,128)(2,1)} %shard_map.64) | data formatting | bytes 2097152

commit v2 on v1

--- a/solution.py
+++ b/solution.py
@@ -88,8 +88,8 @@
         def _():
             c_in[o] = jnp.zeros(c_in.shape[1:], BF16)
 
-    for slot in range(3):
-        @pl.when(pos < slot + 2)
+    for slot in range(2):
+        @pl.when(pos < 2 * slot + 2)
         def _():
             med_in[slot] = jnp.zeros(med_in.shape[1:], BF16)
 
@@ -120,10 +120,9 @@
 
     def med_copy(slot):
         src = med_own if slot == 0 else med_in.at[0]
-        step = (2, 1, 2)[slot]
         return remote(
             src, med_in.at[slot], med_ss.at[slot], med_rs.at[slot],
-            seq=jnp.minimum(pos + step, n_seq - 1),
+            seq=jnp.minimum(pos + 2, n_seq - 1),
         )
 
     def c_copy(to):
@@ -176,11 +175,16 @@
 
             @pl.loop(0, heads)
             def _(h):
-                s = mm_nt(k_v[:, hs(h)], q_in[i, :, hs(h)])
-                m = jnp.max(s, axis=0, keepdims=True)
+                q = q_in[i, :, hs(h)]
+                s = mm_nt(k_v[:, hs(h)], q)
+                s2 = jnp.where(pos >= 2, mm_nt(med_in[0, 0, h], q), -jnp.inf)
+                m = jnp.maximum(
+                    jnp.max(s, axis=0, keepdims=True), jnp.max(s2, axis=0, keepdims=True)
+                )
                 p = jnp.exp((s - m) * scale)
-                total = jnp.sum(p, axis=0, keepdims=True)
-                o = mm(vt[h], p.astype(BF16))
+                p2 = jnp.exp((s2 - m) * scale)
+                total = jnp.sum(p, axis=0, keepdims=True) + jnp.sum(p2, axis=0, keepdims=True)
+                o = mm(vt[h], p.astype(BF16)) + mm(med_in[0, 1, h], p2.astype(BF16))
                 oe_out[i, h] = (o / total).astype(BF16)
                 le_out[i, h] = m * scale + jnp.log(total)
                 oe_copy(i, h).start()
@@ -198,9 +202,9 @@
             key_at = lax.broadcasted_iota(jnp.int32, (keys, chunk), 0)
             query_at = lax.broadcasted_iota(jnp.int32, (keys, chunk), 1) + first
             parts = [(jnp.where(key_at <= query_at, s, -jnp.inf), vt[h, :, pl.ds(0, keys)])]
-            for slot in range(3):
+            for slot in range(2):
                 s = mm_nt(med_in[slot, 0, h], q)
-                parts.append((jnp.where(pos >= slot + 2, s, -jnp.inf), med_in[slot, 1, h]))
+                parts.append((jnp.where(pos >= 2 * slot + 2, s, -jnp.inf), med_in[slot, 1, h]))
             s = mm_nt(ck[h], q)
             owner = lax.broadcasted_iota(jnp.int32, s.shape, 0) // n_coarse
             parts.append((jnp.where(owner < pos, s, -jnp.inf), cvt[h]))
@@ -279,21 +283,15 @@
 
         project(i, hd, put_own)
 
-    edge(0)
-
     @pl.when(pos >= 2)
     def _():
         med_copy(0).wait_recv()
 
-        @pl.when(has_next)
+        @pl.when(pos + 2 < n_seq)
         def _():
             med_copy(1).start()
 
-        @pl.when(pos + 2 < n_seq)
-        def _():
-            med_copy(2).start()
-
-    for i in range(1, CHUNKS):
+    for i in range(CHUNKS):
         edge(i)
 
     @pl.loop(0, n_seq)
@@ -309,15 +307,14 @@
         cvt[h] = got[:, n_coarse:].reshape(n_seq * n_coarse, HEAD_DIM).T.astype(BF16)
 
     loads[2].wait()
-    for slot in (1, 2):
-        @pl.when(pos >= slot + 2)
-        def _():
-            med_copy(slot).wait_recv()
-
+
+    @pl.when(pos >= 4)
+    def _():
+        med_copy(1).wait_recv()
+
+    loads[3].wait()
     for i in range(CHUNKS):
         local(i)
-    loads[3].wait()
-    for i in range(CHUNKS):
         combine(i)
         mix(i)
     for i in range(CHUNKS):
@@ -346,13 +343,9 @@
     def _():
         med_copy(0).wait_send()
 
-    @pl.when((pos >= 2) & has_next)
+    @pl.when((pos >= 2) & (pos + 2 < n_seq))
     def _():
         med_copy(1).wait_send()
-
-    @pl.when((pos >= 2) & (pos + 2 < n_seq))
-    def _():
-        med_copy(2).wait_send()
 
     @pl.loop(0, n_seq)
     def _(to):
@@ -392,7 +385,7 @@
         V((CHUNKS, heads, HEAD_DIM, chunk), BF16),
         V((CHUNKS, heads, 1, chunk), F32),
         V((2, heads, n_med, HEAD_DIM), BF16),
-        V((3, 2, heads, n_med, HEAD_DIM), BF16),
+        V((2, 2, heads, n_med, HEAD_DIM), BF16),
         V((heads, 2 * n_coarse, HEAD_DIM), BF16),
         V((n_seq, heads, 2 * n_coarse, HEAD_DIM), BF16),
         V((heads, n_seq * n_coarse, HEAD_DIM), BF16),
@@ -410,7 +403,7 @@
         dma((CHUNKS,)), dma((CHUNKS,)),
         dma((CHUNKS, heads)), dma((CHUNKS, heads)),
         dma((CHUNKS,)), dma((CHUNKS,)),
-        dma((3,)), dma((3,)),
+        dma((2,)), dma((2,)),
         dma((n_seq,)), dma((n_seq,)),
         dma((CHUNKS, groups)), dma((CHUNKS, groups)),
         dma((CHUNKS, far)), dma((CHUNKS, far)),

time: 108 us -> 98.9 us (0.916)
  the two profiles are of different devices: /device:TPU:19 before, /device:TPU:8 now
where the time goes in v2:
time: 98.9 us; the launch traced here: 98.7 us
  Pallas kernels  93.1 us (94%)
  local copies, waits for them, and re-layouts  5.51 us (6%)
    pallas_call x1, Pallas kernels, body(): pl.pallas_call(functools.partial(kernel, n_seq, n_head), out_shape=jax.Sh...  93.1 us
    unnamed x2, local copies, waits for them, and re-layouts  2.95 us

profile of v2, /device:TPU:8, one launch (start us, length us, event | category | flops | bytes accessed | tf_op | source)
XLA Modules:
  0.0 98.7 jit_solution(17421288573378883329)
XLA Ops:
  0.0 0.7 copy.8
  0.7 0.7 tile.18
  1.4 0.7 tile.19.wc_ref
  2.1 0.1 tile.16
  2.2 0.3 tile.17
  2.5 0.7 copy.9.wm_ref
  3.3 93.1 %shard_map.64 = bf16[512,1024]{1,0:T(8,128)(2,1)} custom-call(bf16[512,1024]{1,0:T(8,128)(2,1)} %q_hbm.1, bf16[512,1024]{1,0:T(8,128)(2,1)} %k_hbm.1, bf16[512,1024]{1,0:T(8,128)(2,1)} %v_hbm.1, f32[16,1,512]{2,1,0:T(1,128)} %copy.9.wm_ref, f32[16,1,512]{2,1,0:T(1,128)} %tile.19.wc_ref, bf16[1024,4096]{1,0:T(8,128)(2,1)} %w_hbm.1), custom_call_target="tpu_custom_call" | custom-call | tf_op jit(solution)/shard_map/pallas_call | solution.py:411
  96.4 2.3 %copy.11 = bf16[512,1024]{1,0:T(8,128)(2,1)} copy(bf16[512,1024]{1,0:T(8,128)(2,1)} %shard_map.64) | data formatting | bytes 2097152
